TPU v7x, 512 devices: a whole 4x4x16 slice. The times are simulated.
512 devices in a mesh: task: 4 (over z_hi, core), seq: 16 (over x, y), dp: 8 (over z_lo).
Axes of the slice: x: 4, y: 4, z: 16 (z_hi: 2, z_lo: 8; z = z_hi * 8 + z_lo), core: 2. Of those that a mesh axis runs over, the one named last changes fastest.
Arguments:
- enc_grads: bfloat16 [4, 8, 2048, 4096], P('task', 'dp', 'seq'), may hold values from -12 to 12
- hidden: bfloat16 [8, 2048, 4096], P('dp', 'seq', 'task'), may hold values from -900 to 900
- final_gain: float32 [4096], replicated, may hold values from 0.1 to 1.9
- attn_out: bfloat16 [8, 2048, 4096], P('dp', 'seq', 'task'), may hold values from -6 to 6
- qkv: bfloat16 [8, 2048, 64, 192], P('dp', None, ('task', 'seq')), may hold values from -48 to 48
- out_weight: bfloat16 [4096, 4096], P('task', ('seq', 'dp')), may hold values from -0.09375 to 0.09375
- doc_lengths: int32 [8], P('dp'), may hold values from 512 to 2048
Outputs:
- resid_grad: bfloat16 [8, 2048, 4096], P('dp', 'seq', 'task')
- qkv_grad: bfloat16 [8, 2048, 64, 192], P('dp', None, ('task', 'seq'))
- weight_grad: float32 [4096, 4096], P('task', ('seq', 'dp'))
Inputs may be any that keep to these rules, and one draw needn't show every extreme that they name: `doc_lengths`: positions at or after a document's length are padding and are never attended to as keys.
All inputs are finite; a program needn't handle non-finite values.
Results may differ from a plain program's by a relative error of at most 0.02.
Values may be sent and summed in bfloat16 or wider, within the bound.
No kernel may reach another device: no remote copies, remote signals or barrier semaphores. Data moves between devices by JAX's collectives and lax.ppermute only.
A program may use at most 64 MiB of HBM per device.

v0:
```python
import jax
import jax.numpy as jnp
from jax import lax
from jax.sharding import PartitionSpec as P

eps_norm = 1e-06


def split_up(shard, dim, peers):
    lengths = shard.shape
    pieces = shard.reshape(*lengths[:dim], peers, lengths[dim] // peers, *lengths[dim + 1 :])
    return jnp.moveaxis(pieces, dim, 0)


def sent_and_summed(shard, axis, dim):
    pieces = split_up(shard, dim, lax.axis_size(axis))
    arrived = lax.all_to_all(pieces, axis, split_axis=0, concat_axis=0, tiled=True)
    return arrived.astype(jnp.float32).sum(axis=0)


def copy_for_each(shard, axis):
    copies = jnp.broadcast_to(shard, (lax.axis_size(axis), *shard.shape))
    return lax.all_to_all(copies, axis, split_axis=0, concat_axis=0, tiled=True)


def over_copies(shard, axis):
    everything = copy_for_each(shard, axis)
    return jnp.sum(everything, axis=0)


def packed_total(arrays, axis):
    ends = [0]
    for a in arrays:
        ends.append(ends[-1] + a.size)
    running = over_copies(jnp.concatenate([a.ravel() for a in arrays]), axis)
    return tuple((running[b:e].reshape(a.shape) for a, b, e in zip(arrays, ends, ends[1:])))


def joined_along(pieces, dim):
    lengths = list(pieces.shape[1:])
    lengths[dim] *= pieces.shape[0]
    return jnp.moveaxis(pieces, 0, dim).reshape(lengths)


def gather_directly(shard, axis, dim):
    return joined_along(copy_for_each(shard, axis), dim)


def on_device(enc_grads, hidden, final_gain, attn_out, qkv, out_weight, doc_lengths):
    feature_cols = enc_grads.shape[3]
    task_count = lax.axis_size("task")
    task_pos = lax.axis_index("task")
    share_cols = feature_cols // task_count
    partial_terms = enc_grads[0, 0].astype(jnp.float32)
    summed = sent_and_summed(partial_terms.astype(jnp.bfloat16), "task", 1)
    rows_part = hidden[0].astype(jnp.float32)
    gain_part = lax.dynamic_slice_in_dim(final_gain, task_pos * share_cols, share_cols, 0)
    squares, cross_sum = packed_total(
        (jnp.sum(rows_part * rows_part, axis=-1), jnp.sum(gain_part * summed * rows_part, axis=-1)),
        "task",
    )
    scale_inv = lax.rsqrt(squares / feature_cols + eps_norm)[:, None]
    cross_mean = cross_sum[:, None] * scale_inv / feature_cols
    resid_part = (scale_inv * (gain_part * summed - rows_part * scale_inv * cross_mean)).astype(
        jnp.bfloat16
    )
    resid_full = gather_directly(resid_part, "task", 1)
    weight_slab = gather_directly(out_weight, "dp", 1)
    resid_slice = resid_full
    head_grad = lax.dot_general(
        resid_slice,
        lax.all_gather(weight_slab, "seq", axis=1, tiled=True),
        (((1,), (1,)), ((), ())),
        preferred_element_type=jnp.float32,
    )
    head_grad = head_grad.astype(jnp.bfloat16)
    saved_tok = attn_out[0]
    out_heads, saved_heads = (
        lax.all_to_all(head_grad, "seq", split_axis=1, concat_axis=0, tiled=True),
        lax.all_to_all(saved_tok, "seq", split_axis=1, concat_axis=0, tiled=True),
    )
    resid_cols = lax.all_to_all(resid_full, "seq", split_axis=1, concat_axis=0, tiled=True)
    resid_slice = resid_cols
    grad_block = lax.dot_general(
        lax.all_gather(saved_tok, "seq", axis=0, tiled=True),
        resid_slice,
        (((0,), (0,)), ((), ())),
        preferred_element_type=jnp.float32,
    )
    seq_len = qkv.shape[1]
    weight_grad = sent_and_summed(grad_block.astype(jnp.bfloat16), "dp", 1)
    head_size = qkv.shape[3] // 3
    doc_length = doc_lengths[0]
    key_valid = (jnp.arange(seq_len, dtype=jnp.int32) < doc_length)[None, :]
    block_rows = min(512, seq_len)
    block_count = seq_len // block_rows
    query = qkv[0, :, 0, :head_size]
    key_rows = qkv[0, :, 0, head_size : 2 * head_size]
    value_rows = qkv[0, :, 0, 2 * head_size :]
    delta_rows = jnp.sum(out_heads.astype(jnp.float32) * saved_heads.astype(jnp.float32), axis=-1)

    def block_step(state_pair, block_index):
        key_acc, value_acc = state_pair
        row_start = block_index * block_rows
        query_blk = lax.dynamic_slice_in_dim(query, row_start, block_rows, 0)
        upstream_blk = lax.dynamic_slice_in_dim(out_heads, row_start, block_rows, 0)
        delta_blk = lax.dynamic_slice_in_dim(delta_rows, row_start, block_rows, 0)
        scores = lax.dot_general(
            query_blk, key_rows, (((1,), (1,)), ((), ())), preferred_element_type=jnp.float32
        )
        scores = jnp.where(key_valid, scores, -1e30)
        row_max = jnp.max(scores, axis=-1, keepdims=True)
        expo_terms = jnp.exp(scores - row_max)
        prob_rows = expo_terms / jnp.sum(expo_terms, axis=-1, keepdims=True)
        prob_bf16 = prob_rows.astype(jnp.bfloat16)
        value_acc = value_acc + lax.dot_general(
            prob_bf16, upstream_blk, (((0,), (0,)), ((), ())), preferred_element_type=jnp.float32
        )
        dprob_rows = lax.dot_general(
            upstream_blk, value_rows, (((1,), (1,)), ((), ())), preferred_element_type=jnp.float32
        )
        dscore_rows = (prob_rows * (dprob_rows - delta_blk[:, None])).astype(jnp.bfloat16)
        dquery = jnp.dot(dscore_rows, key_rows, preferred_element_type=jnp.float32).astype(
            jnp.bfloat16
        )
        key_acc = key_acc + lax.dot_general(
            dscore_rows, query_blk, (((0,), (0,)), ((), ())), preferred_element_type=jnp.float32
        )
        return ((key_acc, value_acc), dquery)

    zero_pair = (
        jnp.zeros((seq_len, head_size), jnp.float32),
        jnp.zeros((seq_len, head_size), jnp.float32),
    )
    (key_acc, value_acc), dq_blocks = lax.scan(
        block_step, zero_pair, jnp.arange(block_count, dtype=jnp.int32)
    )
    dquery_all = dq_blocks.reshape(seq_len, head_size)
    head_grads = [
        jnp.concatenate(
            [dquery_all, key_acc.astype(jnp.bfloat16), value_acc.astype(jnp.bfloat16)], axis=-1
        )
    ]
    qkv_grad = jnp.stack(head_grads, axis=1)[None]
    return (resid_part[None], qkv_grad, weight_grad)


def solution(mesh):
    return jax.shard_map(
        on_device,
        mesh=mesh,
        in_specs=(
            P("task", "dp", "seq", None),
            P("dp", "seq", "task"),
            P(),
            P("dp", "seq", "task"),
            P("dp", None, ("task", "seq"), None),
            P("task", ("seq", "dp")),
            P("dp"),
        ),
        out_specs=(
            P("dp", "seq", "task"),
            P("dp", None, ("task", "seq"), None),
            P("task", ("seq", "dp")),
        ),
        check_vma=False,
    )
```

profile of v0, /device:TPU:8, one launch (start us, length us, event | category | flops | bytes accessed | tf_op | source)
XLA Modules:
  0.0 326.9 jit_solution(1640961790241758674)
XLA Ops:
  8.8 41.2 %all_to_all.77 = bf16[8,1024,32]{1,2,0:T(8,128)(2,1)} all-to-all(bf16[8,1024,32]{1,2,0:T(8,128)(2,1)S(1)} %broadcast_in_dim.42), channel_id=1, replica_groups=mesh['task'=4,'seq'=16,'dp'=8] {'dp'}, dimensions={0} | all-to-all | bytes 1048576 | tf_op jit(solution)/shard_map/all_to_all | solution.py:23
  50.0 1.7 copy.68
  53.1 7.6 %all-to-all-start = ((bf16[4,128,1024]{2,1,0:T(8,128)(2,1)}), bf16[4,128,1024]{2,1,0:T(8,128)(2,1)S(1)}, u32[]{:S(2)}, u32[]{:S(2)}) async-start(bf16[4,128,1024]{2,1,0:T(8,128)(2,1)} %copy.69), calls=%async_computation | async-start | bytes 2097152 | tf_op jit(solution)/shard_map/all_to_all | solution.py:17
  61.3 44.1 %all-to-all-done = bf16[4,128,1024]{2,1,0:T(8,128)(2,1)S(1)} async-done(((bf16[4,128,1024]{2,1,0:T(8,128)(2,1)}), bf16[4,128,1024]{2,1,0:T(8,128)(2,1)S(1)}, u32[]{:S(2)}, u32[]{:S(2)}) %all-to-all-start) | async-done | bytes 1048608 | tf_op jit(solution)/shard_map/all_to_all | solution.py:17
  105.8 14.8 %all_to_all.78 = f32[4,1,256]{2,1,0:T(1,128)S(1)} all-to-all(f32[4,1,256]{2,1,0:T(1,128)S(1)} %broadcast_in_dim.39), channel_id=1, replica_groups=mesh['task'=4,'seq'=16,'dp'=8] {'task'}, dimensions={0} | all-to-all | bytes 8192 | tf_op jit(solution)/shard_map/all_to_all | solution.py:23
  121.2 30.5 %all_to_all.79 = bf16[4,128,1024]{1,2,0:T(8,128)(2,1)S(1)} all-to-all(bf16[4,128,1024]{1,2,0:T(8,128)(2,1)S(1)} %broadcast_in_dim.41), channel_id=1, replica_groups=mesh['task'=4,'seq'=16,'dp'=8] {'task'}, dimensions={0} | all-to-all | bytes 2097152 | tf_op jit(solution)/shard_map/all_to_all | solution.py:23
  151.8 30.4 %all_to_all.80 = bf16[128,16,256]{0,2,1:T(8,128)(2,1)S(1)} all-to-all(bf16[128,16,256]{0,2,1:T(8,128)(2,1)S(1)} %bitcast.93), channel_id=1, replica_groups=mesh['task'=4,'seq'=16,'dp'=8] {'seq'}, dimensions={1} | all-to-all | bytes 2097152 | tf_op jit(solution)/shard_map/all_to_all | solution.py:82
  183.5 4.6 %fusion.19 = bf16[256,1024]{1,0:T(8,128)(2,1)} fusion(bf16[2048,256]{1,0:T(8,128)(2,1)} %bitcast.100, bf16[1,2048,1024]{2,1,0:T(8,128)(2,1)} %all-gather.6.cloned.1.call-done), kind=kOutput, calls=%fused_computation.25 | convolution fusion | flops 1074003968 | bytes 5767168 | tf_op jit(solution)/shard_map/dot_general | solution.py:84
  188.1 25.5 %all-to-all-start.7 = ((bf16[8,1024,32]{1,2,0:T(8,128)(2,1)}), bf16[8,1024,32]{1,2,0:T(8,128)(2,1)S(1)}, u32[]{:S(2)}, u32[]{:S(2)}) async-start(bf16[8,1024,32]{1,2,0:T(8,128)(2,1)} %bitcast.25), calls=%async_computation.7 | async-start | bytes 1048576 | tf_op jit(solution)/shard_map/all_to_all | solution.py:17
  214.5 4.7 %convolution_convert_fusion.1 = bf16[128,1024]{1,0:T(8,128)(2,1)S(1)} fusion(bf16[128,4096]{0,1:T(8,128)(2,1)S(1)} %bitcast.94, bf16[1024,4096]{0,1:T(8,128)(2,1)} %all-gather.4.cloned.1.call-done), kind=kOutput, calls=%fused_computation.26 | convolution fusion | flops 1073872896 | bytes 9699328 | tf_op jit(solution)/shard_map/dot_general | solution.py:70
  220.0 21.6 %all-to-all-done.7 = bf16[8,1024,32]{1,2,0:T(8,128)(2,1)S(1)} async-done(((bf16[8,1024,32]{1,2,0:T(8,128)(2,1)}), bf16[8,1024,32]{1,2,0:T(8,128)(2,1)S(1)}, u32[]{:S(2)}, u32[]{:S(2)}) %all-to-all-start.7) | async-done | bytes 524320 | tf_op jit(solution)/shard_map/all_to_all | solution.py:17
  241.6 5.1 %all-to-all-start.4 = ((bf16[128,16,64]{0,2,1:T(8,128)(2,1)}), bf16[128,16,64]{0,2,1:T(8,128)(2,1)S(1)}, u32[]{:S(2)}, u32[]{:S(2)}) async-start(bf16[128,16,64]{0,2,1:T(8,128)(2,1)} %bitcast.10), calls=%async_computation.4 | async-start | bytes 524288 | tf_op jit(solution)/shard_map/all_to_all | solution.py:79
  249.4 4.6 %all-to-all-done.4 = bf16[128,16,64]{0,2,1:T(8,128)(2,1)S(1)} async-done(((bf16[128,16,64]{0,2,1:T(8,128)(2,1)}), bf16[128,16,64]{0,2,1:T(8,128)(2,1)S(1)}, u32[]{:S(2)}, u32[]{:S(2)}) %all-to-all-start.4) | async-done | bytes 262176 | tf_op jit(solution)/shard_map/all_to_all | solution.py:79
  254.1 5.1 %all-to-all-start.5 = ((bf16[128,16,64]{0,2,1:T(8,128)(2,1)}), bf16[128,16,64]{0,2,1:T(8,128)(2,1)S(1)}, u32[]{:S(2)}, u32[]{:S(2)}) async-start(bf16[128,16,64]{0,2,1:T(8,128)(2,1)} %bitcast.14), calls=%async_computation.5 | async-start | bytes 524288 | tf_op jit(solution)/shard_map/all_to_all | solution.py:80
  261.1 5.0 %all-to-all-done.5 = bf16[128,16,64]{0,2,1:T(8,128)(2,1)S(1)} async-done(((bf16[128,16,64]{0,2,1:T(8,128)(2,1)}), bf16[128,16,64]{0,2,1:T(8,128)(2,1)S(1)}, u32[]{:S(2)}, u32[]{:S(2)}) %all-to-all-start.5) | async-done | bytes 262176 | tf_op jit(solution)/shard_map/all_to_all | solution.py:80
  266.2 50.8 %while.15 = (s32[]{:T(128)}, f32[2048,64]{0,1:T(8,128)S(1)}, f32[2048,64]{0,1:T(8,128)}, bf16[4,512,64]{1,2,0:T(8,128)(2,1)}, s32[4]{0:T(128)S(1)}, /*index=5*/b...) while((s32[]{:T(128)}, f32[2048,64]{0,1:T(8,128)S(1)}, ...), condition=%wide.region_8.9_spmd.clone, body=%wide.region_5.8_spmd.clone.sunk | while | flops 687375360 | bytes 65895284 | solution.py:135
  269.0 1.9 copy-done
  271.8 3.5 %convolution_add_fusion.5 = f32[2048,64]{0,1:T(8,128)S(1)} fusion(f32[2048,64]{0,1:T(8,128)S(1)} %copy-done.5, pred[]{:T(512)S(6)} %compare.3, bf16[2048,64]{1,0:T(8,128)(2,1)S(1)} %get-tuple-element.298, s32[]{:T(128)S(6)} %select_n.35, f32[512,2048]{1,0:T(8,128)} %copy-done, f32[512]{0:T(512)S(1)} %fusion.65, f32[512]{0:T(512)S(1)} %get-tuple-element.260, ...), kind=kOutput, calls=%fused_computation.6.clone.1 | convolution fusion | flops 138674176 | bytes 5380101 | tf_op jit(solution)/shard_map/while/body/eval_jaxpr/dot_general | solution.py:116
  275.3 1.6 multiply_convert_fusion.2
  277.5 1.4 fusion.66
  281.7 1.9 copy-done
  284.5 3.5 %convolution_add_fusion.5 = f32[2048,64]{0,1:T(8,128)S(1)} fusion(f32[2048,64]{0,1:T(8,128)S(1)} %copy-done.5, pred[]{:T(512)S(6)} %compare.3, bf16[2048,64]{1,0:T(8,128)(2,1)S(1)} %get-tuple-element.298, s32[]{:T(128)S(6)} %select_n.35, f32[512,2048]{1,0:T(8,128)} %copy-done, f32[512]{0:T(512)S(1)} %fusion.65, f32[512]{0:T(512)S(1)} %get-tuple-element.260, ...), kind=kOutput, calls=%fused_computation.6.clone.1 | convolution fusion | flops 138674176 | bytes 5380101 | tf_op jit(solution)/shard_map/while/body/eval_jaxpr/dot_general | solution.py:116
  288.0 1.6 multiply_convert_fusion.2
  290.2 1.4 fusion.66
  294.4 1.9 copy-done
  297.1 3.5 %convolution_add_fusion.5 = f32[2048,64]{0,1:T(8,128)S(1)} fusion(f32[2048,64]{0,1:T(8,128)S(1)} %copy-done.5, pred[]{:T(512)S(6)} %compare.3, bf16[2048,64]{1,0:T(8,128)(2,1)S(1)} %get-tuple-element.298, s32[]{:T(128)S(6)} %select_n.35, f32[512,2048]{1,0:T(8,128)} %copy-done, f32[512]{0:T(512)S(1)} %fusion.65, f32[512]{0:T(512)S(1)} %get-tuple-element.260, ...), kind=kOutput, calls=%fused_computation.6.clone.1 | convolution fusion | flops 138674176 | bytes 5380101 | tf_op jit(solution)/shard_map/while/body/eval_jaxpr/dot_general | solution.py:116
  300.7 1.6 multiply_convert_fusion.2
  302.9 1.4 fusion.66
  307.0 1.9 copy-done
  309.8 3.5 %convolution_add_fusion.5 = f32[2048,64]{0,1:T(8,128)S(1)} fusion(f32[2048,64]{0,1:T(8,128)S(1)} %copy-done.5, pred[]{:T(512)S(6)} %compare.3, bf16[2048,64]{1,0:T(8,128)(2,1)S(1)} %get-tuple-element.298, s32[]{:T(128)S(6)} %select_n.35, f32[512,2048]{1,0:T(8,128)} %copy-done, f32[512]{0:T(512)S(1)} %fusion.65, f32[512]{0:T(512)S(1)} %get-tuple-element.260, ...), kind=kOutput, calls=%fused_computation.6.clone.1 | convolution fusion | flops 138674176 | bytes 5380101 | tf_op jit(solution)/shard_map/while/body/eval_jaxpr/dot_general | solution.py:116
  313.4 1.6 multiply_convert_fusion.2
  315.6 1.4 fusion.66
  (101 shorter events, 29.7 us)
Async XLA Ops:
  7.2 176.3 %all-gather.6.cloned.1.call-start = ((), (), s32[]{:S(2)}) async-start(), calls=%async_computation.9 | async-start | bytes 4456448 | tf_op jit(solution)/shard_map/all_gather | solution.py:85
  7.9 206.6 %all-gather.4.cloned.1.call-start = ((), (), s32[]{:S(2)}) async-start(), calls=%async_computation.8 | async-start | bytes 8912896 | tf_op jit(solution)/shard_map/all_gather | solution.py:72
  50.0 55.6 %copy-start.2 = (bf16[1,128,1024]{2,1,0:T(8,128)(2,1)S(1)}, bf16[1,128,1024]{2,1,0:T(8,128)(2,1)}, u32[]{:S(2)}) copy-start(bf16[1,128,1024]{2,1,0:T(8,128)(2,1)} %param.10) | copy-start | bytes 786436
  53.1 52.4 %all-to-all-start = ((bf16[4,128,1024]{2,1,0:T(8,128)(2,1)}), bf16[4,128,1024]{2,1,0:T(8,128)(2,1)S(1)}, u32[]{:S(2)}, u32[]{:S(2)}) async-start(bf16[4,128,1024]{2,1,0:T(8,128)(2,1)} %copy.69), calls=%async_computation | async-start | bytes 2097152 | tf_op jit(solution)/shard_map/all_to_all | solution.py:17
  183.5 30.1 %copy-start.3 = (bf16[1,128,1024]{2,1,0:T(8,128)(2,1)S(1)}, bf16[1,128,1024]{2,1,0:T(8,128)(2,1)}, u32[]{:S(2)}) copy-start(bf16[1,128,1024]{2,1,0:T(8,128)(2,1)} %param.12) | copy-start | bytes 786436
  188.1 53.5 %all-to-all-start.7 = ((bf16[8,1024,32]{1,2,0:T(8,128)(2,1)}), bf16[8,1024,32]{1,2,0:T(8,128)(2,1)S(1)}, u32[]{:S(2)}, u32[]{:S(2)}) async-start(bf16[8,1024,32]{1,2,0:T(8,128)(2,1)} %bitcast.25), calls=%async_computation.7 | async-start | bytes 1048576 | tf_op jit(solution)/shard_map/all_to_all | solution.py:17
  241.6 12.5 %all-to-all-start.4 = ((bf16[128,16,64]{0,2,1:T(8,128)(2,1)}), bf16[128,16,64]{0,2,1:T(8,128)(2,1)S(1)}, u32[]{:S(2)}, u32[]{:S(2)}) async-start(bf16[128,16,64]{0,2,1:T(8,128)(2,1)} %bitcast.10), calls=%async_computation.4 | async-start | bytes 524288 | tf_op jit(solution)/shard_map/all_to_all | solution.py:79
  254.1 12.1 %all-to-all-start.5 = ((bf16[128,16,64]{0,2,1:T(8,128)(2,1)}), bf16[128,16,64]{0,2,1:T(8,128)(2,1)S(1)}, u32[]{:S(2)}, u32[]{:S(2)}) async-start(bf16[128,16,64]{0,2,1:T(8,128)(2,1)} %bitcast.14), calls=%async_computation.5 | async-start | bytes 524288 | tf_op jit(solution)/shard_map/all_to_all | solution.py:80
  268.2 3.6 %copy-start.5 = (f32[2048,64]{0,1:T(8,128)S(1)}, f32[2048,64]{0,1:T(8,128)}, u32[]{:S(2)}) copy-start(f32[2048,64]{0,1:T(8,128)} %get-tuple-element.278) | copy-start | bytes 1572868 | tf_op jit(solution)/shard_map/while
  269.0 1.9 copy-start
  271.7 3.6 %copy-start.1 = (f32[512,2048]{1,0:T(8,128)S(1)}, f32[512,2048]{1,0:T(8,128)}, u32[]{:S(2)}) copy-start(f32[512,2048]{1,0:T(8,128)} %copy-done) | copy-start | bytes 12582916 | tf_op jit(solution)/shard_map/while
  271.8 3.6 %copy-start.4 = (bf16[2048,64]{1,0:T(8,128)(2,1)S(1)}, bf16[2048,64]{1,0:T(8,128)(2,1)}, u32[]{:S(2)}) copy-start(bf16[2048,64]{1,0:T(8,128)(2,1)} %get-tuple-element.299) | copy-start | bytes 786436 | tf_op jit(solution)/shard_map/while
  275.2 1.7 copy-start.6
  280.9 3.6 %copy-start.5 = (f32[2048,64]{0,1:T(8,128)S(1)}, f32[2048,64]{0,1:T(8,128)}, u32[]{:S(2)}) copy-start(f32[2048,64]{0,1:T(8,128)} %get-tuple-element.278) | copy-start | bytes 1572868 | tf_op jit(solution)/shard_map/while
  281.7 1.9 copy-start
  284.4 3.6 %copy-start.1 = (f32[512,2048]{1,0:T(8,128)S(1)}, f32[512,2048]{1,0:T(8,128)}, u32[]{:S(2)}) copy-start(f32[512,2048]{1,0:T(8,128)} %copy-done) | copy-start | bytes 12582916 | tf_op jit(solution)/shard_map/while
  284.5 3.6 %copy-start.4 = (bf16[2048,64]{1,0:T(8,128)(2,1)S(1)}, bf16[2048,64]{1,0:T(8,128)(2,1)}, u32[]{:S(2)}) copy-start(bf16[2048,64]{1,0:T(8,128)(2,1)} %get-tuple-element.299) | copy-start | bytes 786436 | tf_op jit(solution)/shard_map/while
  287.9 1.7 copy-start.6
  293.6 3.6 %copy-start.5 = (f32[2048,64]{0,1:T(8,128)S(1)}, f32[2048,64]{0,1:T(8,128)}, u32[]{:S(2)}) copy-start(f32[2048,64]{0,1:T(8,128)} %get-tuple-element.278) | copy-start | bytes 1572868 | tf_op jit(solution)/shard_map/while
  294.4 1.9 copy-start
  297.1 3.6 %copy-start.1 = (f32[512,2048]{1,0:T(8,128)S(1)}, f32[512,2048]{1,0:T(8,128)}, u32[]{:S(2)}) copy-start(f32[512,2048]{1,0:T(8,128)} %copy-done) | copy-start | bytes 12582916 | tf_op jit(solution)/shard_map/while
  297.1 3.6 %copy-start.4 = (bf16[2048,64]{1,0:T(8,128)(2,1)S(1)}, bf16[2048,64]{1,0:T(8,128)(2,1)}, u32[]{:S(2)}) copy-start(bf16[2048,64]{1,0:T(8,128)(2,1)} %get-tuple-element.299) | copy-start | bytes 786436 | tf_op jit(solution)/shard_map/while
  300.6 1.7 copy-start.6
  306.2 3.6 %copy-start.5 = (f32[2048,64]{0,1:T(8,128)S(1)}, f32[2048,64]{0,1:T(8,128)}, u32[]{:S(2)}) copy-start(f32[2048,64]{0,1:T(8,128)} %get-tuple-element.278) | copy-start | bytes 1572868 | tf_op jit(solution)/shard_map/while
  307.0 1.9 copy-start
  309.8 3.6 %copy-start.1 = (f32[512,2048]{1,0:T(8,128)S(1)}, f32[512,2048]{1,0:T(8,128)}, u32[]{:S(2)}) copy-start(f32[512,2048]{1,0:T(8,128)} %copy-done) | copy-start | bytes 12582916 | tf_op jit(solution)/shard_map/while
  309.8 3.6 %copy-start.4 = (bf16[2048,64]{1,0:T(8,128)(2,1)S(1)}, bf16[2048,64]{1,0:T(8,128)(2,1)}, u32[]{:S(2)}) copy-start(bf16[2048,64]{1,0:T(8,128)(2,1)} %get-tuple-element.299) | copy-start | bytes 786436 | tf_op jit(solution)/shard_map/while
  313.3 1.7 copy-start.6
Sparse Core Ops, SparseCore 0:
  11.0 70.9 all-gather.5
  85.0 96.0 all-gather.3
where the time goes:
time: 328 us; the launch traced here: 327 us
  blocking collectives  117 us (36%)
  waiting for transfers between devices  76.1 us (23%)
  starting transfers between devices  43.4 us (13%)
  matrix products  40.7 us (12%)
  local copies, waits for them, and re-layouts  22.4 us (7%)
  between operations  14.2 us (4%)
  other arithmetic  10.4 us (3%)
    all_to_all x3, blocking collectives, copy_for_each(): return lax.all_to_all(copies, axis, split_axis=0, concat_axis=0, tiled=True)  86.5 us
    all_to_all x2, waiting for transfers between devices, sent_and_summed(): lax.all_to_all(pieces, axis, split_axis=0, concat_axis=0, tiled=True)  65.7 us
    all_to_all x2, starting transfers between devices, sent_and_summed(): lax.all_to_all(pieces, axis, split_axis=0, concat_axis=0, tiled=True)  33.1 us
    all_to_all x1, blocking collectives, on_device(): lax.all_to_all(resid_full, 'seq', split_axis=1, concat_axis=0, tiled=True)  30.4 us
    dot_general x4, matrix products, block_step(): lax.dot_general(prob_bf16, upstream_blk, (((0,), (0,)), ((), ())), prefer...  13.8 us
    while x40, local copies, waits for them, and re-layouts  7.78 us
  transfers between devices with their start and end apart: 6, of which 4 were waited for; matrix products, arithmetic and copies ran while one was open for 7% of the time, Pallas kernels for 0%

commit v1 on v0

--- a/solution.py
+++ b/solution.py
@@ -79,7 +79,10 @@
         lax.all_to_all(head_grad, "seq", split_axis=1, concat_axis=0, tiled=True),
         lax.all_to_all(saved_tok, "seq", split_axis=1, concat_axis=0, tiled=True),
     )
-    resid_cols = lax.all_to_all(resid_full, "seq", split_axis=1, concat_axis=0, tiled=True)
+    size = lax.axis_size("seq")
+    blocks = jnp.stack(jnp.split(resid_full, size, axis=1), axis=0)
+    blocks = lax.all_to_all(blocks, "seq", split_axis=0, concat_axis=0)
+    resid_cols = jnp.concatenate(blocks, axis=0)
     resid_slice = resid_cols
     grad_block = lax.dot_general(
         lax.all_gather(saved_tok, "seq", axis=0, tiled=True),

time: 328 us -> 328 us (level)
  no operation moved by 1% of the time
where the time goes in v1:
time: 328 us; the launch traced here: 327 us
  blocking collectives  117 us (36%)
  waiting for transfers between devices  76.1 us (23%)
  starting transfers between devices  43.7 us (13%)
  matrix products  40.7 us (12%)
  local copies, waits for them, and re-layouts  22.6 us (7%)
  between operations  14.2 us (4%)
  other arithmetic  10.4 us (3%)
    all_to_all x3, blocking collectives, copy_for_each(): return lax.all_to_all(copies, axis, split_axis=0, concat_axis=0, tiled=True)  86.5 us
    all_to_all x2, waiting for transfers between devices, sent_and_summed(): lax.all_to_all(pieces, axis, split_axis=0, concat_axis=0, tiled=True)  65.7 us
    all_to_all x2, starting transfers between devices, sent_and_summed(): lax.all_to_all(pieces, axis, split_axis=0, concat_axis=0, tiled=True)  33.4 us
    all_to_all x1, blocking collectives, on_device(): blocks = lax.all_to_all(blocks, 'seq', split_axis=0, concat_axis=0)  30.1 us
    dot_general x4, matrix products, block_step(): lax.dot_general(prob_bf16, upstream_blk, (((0,), (0,)), ((), ())), prefer...  13.8 us
    while x40, local copies, waits for them, and re-layouts  7.78 us
  transfers between devices with their start and end apart: 6, of which 4 were waited for; matrix products, arithmetic and copies ran while one was open for 7% of the time, Pallas kernels for 0%

profile of v1, /device:TPU:8, one launch (start us, length us, event | category | flops | bytes accessed | tf_op | source)
XLA Modules:
  0.0 327.2 jit_solution(11421948936153894410)
XLA Ops:
  8.8 41.2 %all_to_all.63 = bf16[8,1024,32]{1,2,0:T(8,128)(2,1)} all-to-all(bf16[8,1024,32]{1,2,0:T(8,128)(2,1)S(1)} %broadcast_in_dim.42), channel_id=1, replica_groups=mesh['task'=4,'seq'=16,'dp'=8] {'dp'}, dimensions={0} | all-to-all | bytes 1048576 | tf_op jit(solution)/shard_map/all_to_all | solution.py:23
  50.0 1.7 copy.67
  53.1 7.6 %all-to-all-start = ((bf16[4,128,1024]{2,1,0:T(8,128)(2,1)}), bf16[4,128,1024]{2,1,0:T(8,128)(2,1)S(1)}, u32[]{:S(2)}, u32[]{:S(2)}) async-start(bf16[4,128,1024]{2,1,0:T(8,128)(2,1)} %copy.68), calls=%async_computation | async-start | bytes 2097152 | tf_op jit(solution)/shard_map/all_to_all | solution.py:17
  61.3 44.1 %all-to-all-done = bf16[4,128,1024]{2,1,0:T(8,128)(2,1)S(1)} async-done(((bf16[4,128,1024]{2,1,0:T(8,128)(2,1)}), bf16[4,128,1024]{2,1,0:T(8,128)(2,1)S(1)}, u32[]{:S(2)}, u32[]{:S(2)}) %all-to-all-start) | async-done | bytes 1048608 | tf_op jit(solution)/shard_map/all_to_all | solution.py:17
  105.8 14.8 %all_to_all.64 = f32[4,1,256]{2,1,0:T(1,128)S(1)} all-to-all(f32[4,1,256]{2,1,0:T(1,128)S(1)} %broadcast_in_dim.39), channel_id=1, replica_groups=mesh['task'=4,'seq'=16,'dp'=8] {'task'}, dimensions={0} | all-to-all | bytes 8192 | tf_op jit(solution)/shard_map/all_to_all | solution.py:23
  121.2 30.5 %all_to_all.65 = bf16[4,128,1024]{1,2,0:T(8,128)(2,1)S(1)} all-to-all(bf16[4,128,1024]{1,2,0:T(8,128)(2,1)S(1)} %broadcast_in_dim.41), channel_id=1, replica_groups=mesh['task'=4,'seq'=16,'dp'=8] {'task'}, dimensions={0} | all-to-all | bytes 2097152 | tf_op jit(solution)/shard_map/all_to_all | solution.py:23
  152.0 30.1 %all_to_all.66 = bf16[16,128,256]{1,2,0:T(8,128)(2,1)S(1)} all-to-all(bf16[16,128,256]{1,2,0:T(8,128)(2,1)S(1)} %fusion.36), channel_id=1, replica_groups=mesh['task'=4,'seq'=16,'dp'=8] {'seq'}, dimensions={0} | all-to-all | bytes 2097152 | tf_op jit(solution)/shard_map/all_to_all | solution.py:84
  183.5 4.6 %fusion.19 = bf16[256,1024]{1,0:T(8,128)(2,1)} fusion(bf16[2048,256]{1,0:T(8,128)(2,1)} %bitcast.175, bf16[1,2048,1024]{2,1,0:T(8,128)(2,1)} %all-gather.6.cloned.1.call-done), kind=kOutput, calls=%fused_computation.25 | convolution fusion | flops 1074003968 | bytes 5767168 | tf_op jit(solution)/shard_map/dot_general | solution.py:87
  188.1 25.8 %all-to-all-start.7 = ((bf16[8,1024,32]{1,2,0:T(8,128)(2,1)}), bf16[8,1024,32]{1,2,0:T(8,128)(2,1)S(1)}, u32[]{:S(2)}, u32[]{:S(2)}) async-start(bf16[8,1024,32]{1,2,0:T(8,128)(2,1)} %bitcast.40), calls=%async_computation.7 | async-start | bytes 1048576 | tf_op jit(solution)/shard_map/all_to_all | solution.py:17
  214.8 4.7 %convolution_convert_fusion.1 = bf16[128,1024]{1,0:T(8,128)(2,1)S(1)} fusion(bf16[128,4096]{0,1:T(8,128)(2,1)S(1)} %bitcast.170, bf16[1024,4096]{0,1:T(8,128)(2,1)} %all-gather.4.cloned.1.call-done), kind=kOutput, calls=%fused_computation.26 | convolution fusion | flops 1073872896 | bytes 9699328 | tf_op jit(solution)/shard_map/dot_general | solution.py:70
  220.3 21.6 %all-to-all-done.7 = bf16[8,1024,32]{1,2,0:T(8,128)(2,1)S(1)} async-done(((bf16[8,1024,32]{1,2,0:T(8,128)(2,1)}), bf16[8,1024,32]{1,2,0:T(8,128)(2,1)S(1)}, u32[]{:S(2)}, u32[]{:S(2)}) %all-to-all-start.7) | async-done | bytes 524320 | tf_op jit(solution)/shard_map/all_to_all | solution.py:17
  241.9 5.1 %all-to-all-start.4 = ((bf16[128,16,64]{0,2,1:T(8,128)(2,1)}), bf16[128,16,64]{0,2,1:T(8,128)(2,1)S(1)}, u32[]{:S(2)}, u32[]{:S(2)}) async-start(bf16[128,16,64]{0,2,1:T(8,128)(2,1)} %bitcast.10), calls=%async_computation.4 | async-start | bytes 524288 | tf_op jit(solution)/shard_map/all_to_all | solution.py:79
  249.7 4.6 %all-to-all-done.4 = bf16[128,16,64]{0,2,1:T(8,128)(2,1)S(1)} async-done(((bf16[128,16,64]{0,2,1:T(8,128)(2,1)}), bf16[128,16,64]{0,2,1:T(8,128)(2,1)S(1)}, u32[]{:S(2)}, u32[]{:S(2)}) %all-to-all-start.4) | async-done | bytes 262176 | tf_op jit(solution)/shard_map/all_to_all | solution.py:79
  254.4 5.1 %all-to-all-start.5 = ((bf16[128,16,64]{0,2,1:T(8,128)(2,1)}), bf16[128,16,64]{0,2,1:T(8,128)(2,1)S(1)}, u32[]{:S(2)}, u32[]{:S(2)}) async-start(bf16[128,16,64]{0,2,1:T(8,128)(2,1)} %bitcast.14), calls=%async_computation.5 | async-start | bytes 524288 | tf_op jit(solution)/shard_map/all_to_all | solution.py:80
  261.4 5.0 %all-to-all-done.5 = bf16[128,16,64]{0,2,1:T(8,128)(2,1)S(1)} async-done(((bf16[128,16,64]{0,2,1:T(8,128)(2,1)}), bf16[128,16,64]{0,2,1:T(8,128)(2,1)S(1)}, u32[]{:S(2)}, u32[]{:S(2)}) %all-to-all-start.5) | async-done | bytes 262176 | tf_op jit(solution)/shard_map/all_to_all | solution.py:80
  266.5 50.7 %while.15 = (s32[]{:T(128)}, f32[2048,64]{0,1:T(8,128)S(1)}, f32[2048,64]{0,1:T(8,128)}, bf16[4,512,64]{1,2,0:T(8,128)(2,1)}, s32[4]{0:T(128)S(1)}, /*index=5*/b...) while((s32[]{:T(128)}, f32[2048,64]{0,1:T(8,128)S(1)}, ...), condition=%wide.region_8.9_spmd.clone, body=%wide.region_5.8_spmd.clone.sunk | while | flops 687375360 | bytes 65895284 | solution.py:138
  269.3 1.9 copy-done
  272.1 3.5 %convolution_add_fusion.5 = f32[2048,64]{0,1:T(8,128)S(1)} fusion(f32[2048,64]{0,1:T(8,128)S(1)} %copy-done.5, pred[]{:T(512)S(6)} %compare.3, bf16[2048,64]{1,0:T(8,128)(2,1)S(1)} %get-tuple-element.298, s32[]{:T(128)S(6)} %select_n.35, f32[512,2048]{1,0:T(8,128)} %copy-done, f32[512]{0:T(512)S(1)} %fusion.81, f32[512]{0:T(512)S(1)} %get-tuple-element.260, ...), kind=kOutput, calls=%fused_computation.6.clone.1 | convolution fusion | flops 138674176 | bytes 5380101 | tf_op jit(solution)/shard_map/while/body/eval_jaxpr/dot_general | solution.py:119
  275.6 1.6 multiply_convert_fusion.2
  277.8 1.4 fusion.82
  282.0 1.9 copy-done
  284.7 3.5 %convolution_add_fusion.5 = f32[2048,64]{0,1:T(8,128)S(1)} fusion(f32[2048,64]{0,1:T(8,128)S(1)} %copy-done.5, pred[]{:T(512)S(6)} %compare.3, bf16[2048,64]{1,0:T(8,128)(2,1)S(1)} %get-tuple-element.298, s32[]{:T(128)S(6)} %select_n.35, f32[512,2048]{1,0:T(8,128)} %copy-done, f32[512]{0:T(512)S(1)} %fusion.81, f32[512]{0:T(512)S(1)} %get-tuple-element.260, ...), kind=kOutput, calls=%fused_computation.6.clone.1 | convolution fusion | flops 138674176 | bytes 5380101 | tf_op jit(solution)/shard_map/while/body/eval_jaxpr/dot_general | solution.py:119
  288.3 1.6 multiply_convert_fusion.2
  290.5 1.4 fusion.82
  294.7 1.9 copy-done
  297.4 3.5 %convolution_add_fusion.5 = f32[2048,64]{0,1:T(8,128)S(1)} fusion(f32[2048,64]{0,1:T(8,128)S(1)} %copy-done.5, pred[]{:T(512)S(6)} %compare.3, bf16[2048,64]{1,0:T(8,128)(2,1)S(1)} %get-tuple-element.298, s32[]{:T(128)S(6)} %select_n.35, f32[512,2048]{1,0:T(8,128)} %copy-done, f32[512]{0:T(512)S(1)} %fusion.81, f32[512]{0:T(512)S(1)} %get-tuple-element.260, ...), kind=kOutput, calls=%fused_computation.6.clone.1 | convolution fusion | flops 138674176 | bytes 5380101 | tf_op jit(solution)/shard_map/while/body/eval_jaxpr/dot_general | solution.py:119
  301.0 1.6 multiply_convert_fusion.2
  303.2 1.4 fusion.82
  307.3 1.9 copy-done
  310.1 3.5 %convolution_add_fusion.5 = f32[2048,64]{0,1:T(8,128)S(1)} fusion(f32[2048,64]{0,1:T(8,128)S(1)} %copy-done.5, pred[]{:T(512)S(6)} %compare.3, bf16[2048,64]{1,0:T(8,128)(2,1)S(1)} %get-tuple-element.298, s32[]{:T(128)S(6)} %select_n.35, f32[512,2048]{1,0:T(8,128)} %copy-done, f32[512]{0:T(512)S(1)} %fusion.81, f32[512]{0:T(512)S(1)} %get-tuple-element.260, ...), kind=kOutput, calls=%fused_computation.6.clone.1 | convolution fusion | flops 138674176 | bytes 5380101 | tf_op jit(solution)/shard_map/while/body/eval_jaxpr/dot_general | solution.py:119
  313.7 1.6 multiply_convert_fusion.2
  315.9 1.4 fusion.82
  (117 shorter events, 29.9 us)
Async XLA Ops:
  7.2 176.3 %all-gather.6.cloned.1.call-start = ((), (), s32[]{:S(2)}) async-start(), calls=%async_computation.9 | async-start | bytes 4456448 | tf_op jit(solution)/shard_map/all_gather | solution.py:88
  7.9 206.9 %all-gather.4.cloned.1.call-start = ((), (), s32[]{:S(2)}) async-start(), calls=%async_computation.8 | async-start | bytes 8912896 | tf_op jit(solution)/shard_map/all_gather | solution.py:72
  50.0 55.6 %copy-start.2 = (bf16[1,128,1024]{2,1,0:T(8,128)(2,1)S(1)}, bf16[1,128,1024]{2,1,0:T(8,128)(2,1)}, u32[]{:S(2)}) copy-start(bf16[1,128,1024]{2,1,0:T(8,128)(2,1)} %param.10) | copy-start | bytes 786436
  53.1 52.4 %all-to-all-start = ((bf16[4,128,1024]{2,1,0:T(8,128)(2,1)}), bf16[4,128,1024]{2,1,0:T(8,128)(2,1)S(1)}, u32[]{:S(2)}, u32[]{:S(2)}) async-start(bf16[4,128,1024]{2,1,0:T(8,128)(2,1)} %copy.68), calls=%async_computation | async-start | bytes 2097152 | tf_op jit(solution)/shard_map/all_to_all | solution.py:17
  183.5 30.4 %copy-start.3 = (bf16[1,128,1024]{2,1,0:T(8,128)(2,1)S(1)}, bf16[1,128,1024]{2,1,0:T(8,128)(2,1)}, u32[]{:S(2)}) copy-start(bf16[1,128,1024]{2,1,0:T(8,128)(2,1)} %param.12) | copy-start | bytes 786436
  188.1 53.8 %all-to-all-start.7 = ((bf16[8,1024,32]{1,2,0:T(8,128)(2,1)}), bf16[8,1024,32]{1,2,0:T(8,128)(2,1)S(1)}, u32[]{:S(2)}, u32[]{:S(2)}) async-start(bf16[8,1024,32]{1,2,0:T(8,128)(2,1)} %bitcast.40), calls=%async_computation.7 | async-start | bytes 1048576 | tf_op jit(solution)/shard_map/all_to_all | solution.py:17
  241.9 12.5 %all-to-all-start.4 = ((bf16[128,16,64]{0,2,1:T(8,128)(2,1)}), bf16[128,16,64]{0,2,1:T(8,128)(2,1)S(1)}, u32[]{:S(2)}, u32[]{:S(2)}) async-start(bf16[128,16,64]{0,2,1:T(8,128)(2,1)} %bitcast.10), calls=%async_computation.4 | async-start | bytes 524288 | tf_op jit(solution)/shard_map/all_to_all | solution.py:79
  254.4 12.1 %all-to-all-start.5 = ((bf16[128,16,64]{0,2,1:T(8,128)(2,1)}), bf16[128,16,64]{0,2,1:T(8,128)(2,1)S(1)}, u32[]{:S(2)}, u32[]{:S(2)}) async-start(bf16[128,16,64]{0,2,1:T(8,128)(2,1)} %bitcast.14), calls=%async_computation.5 | async-start | bytes 524288 | tf_op jit(solution)/shard_map/all_to_all | solution.py:80
  268.5 3.6 %copy-start.5 = (f32[2048,64]{0,1:T(8,128)S(1)}, f32[2048,64]{0,1:T(8,128)}, u32[]{:S(2)}) copy-start(f32[2048,64]{0,1:T(8,128)} %get-tuple-element.278) | copy-start | bytes 1572868 | tf_op jit(solution)/shard_map/while
  269.3 1.9 copy-start
  272.0 3.6 %copy-start.1 = (f32[512,2048]{1,0:T(8,128)S(1)}, f32[512,2048]{1,0:T(8,128)}, u32[]{:S(2)}) copy-start(f32[512,2048]{1,0:T(8,128)} %copy-done) | copy-start | bytes 12582916 | tf_op jit(solution)/shard_map/while
  272.0 3.6 %copy-start.4 = (bf16[2048,64]{1,0:T(8,128)(2,1)S(1)}, bf16[2048,64]{1,0:T(8,128)(2,1)}, u32[]{:S(2)}) copy-start(bf16[2048,64]{1,0:T(8,128)(2,1)} %get-tuple-element.299) | copy-start | bytes 786436 | tf_op jit(solution)/shard_map/while
  275.5 1.7 copy-start.6
  281.2 3.6 %copy-start.5 = (f32[2048,64]{0,1:T(8,128)S(1)}, f32[2048,64]{0,1:T(8,128)}, u32[]{:S(2)}) copy-start(f32[2048,64]{0,1:T(8,128)} %get-tuple-element.278) | copy-start | bytes 1572868 | tf_op jit(solution)/shard_map/while
  282.0 1.9 copy-start
  284.7 3.6 %copy-start.1 = (f32[512,2048]{1,0:T(8,128)S(1)}, f32[512,2048]{1,0:T(8,128)}, u32[]{:S(2)}) copy-start(f32[512,2048]{1,0:T(8,128)} %copy-done) | copy-start | bytes 12582916 | tf_op jit(solution)/shard_map/while
  284.7 3.6 %copy-start.4 = (bf16[2048,64]{1,0:T(8,128)(2,1)S(1)}, bf16[2048,64]{1,0:T(8,128)(2,1)}, u32[]{:S(2)}) copy-start(bf16[2048,64]{1,0:T(8,128)(2,1)} %get-tuple-element.299) | copy-start | bytes 786436 | tf_op jit(solution)/shard_map/while
  288.2 1.7 copy-start.6
  293.8 3.6 %copy-start.5 = (f32[2048,64]{0,1:T(8,128)S(1)}, f32[2048,64]{0,1:T(8,128)}, u32[]{:S(2)}) copy-start(f32[2048,64]{0,1:T(8,128)} %get-tuple-element.278) | copy-start | bytes 1572868 | tf_op jit(solution)/shard_map/while
  294.6 1.9 copy-start
  297.4 3.6 %copy-start.1 = (f32[512,2048]{1,0:T(8,128)S(1)}, f32[512,2048]{1,0:T(8,128)}, u32[]{:S(2)}) copy-start(f32[512,2048]{1,0:T(8,128)} %copy-done) | copy-start | bytes 12582916 | tf_op jit(solution)/shard_map/while
  297.4 3.6 %copy-start.4 = (bf16[2048,64]{1,0:T(8,128)(2,1)S(1)}, bf16[2048,64]{1,0:T(8,128)(2,1)}, u32[]{:S(2)}) copy-start(bf16[2048,64]{1,0:T(8,128)(2,1)} %get-tuple-element.299) | copy-start | bytes 786436 | tf_op jit(solution)/shard_map/while
  300.9 1.7 copy-start.6
  306.5 3.6 %copy-start.5 = (f32[2048,64]{0,1:T(8,128)S(1)}, f32[2048,64]{0,1:T(8,128)}, u32[]{:S(2)}) copy-start(f32[2048,64]{0,1:T(8,128)} %get-tuple-element.278) | copy-start | bytes 1572868 | tf_op jit(solution)/shard_map/while
  307.3 1.9 copy-start
  310.1 3.6 %copy-start.1 = (f32[512,2048]{1,0:T(8,128)S(1)}, f32[512,2048]{1,0:T(8,128)}, u32[]{:S(2)}) copy-start(f32[512,2048]{1,0:T(8,128)} %copy-done) | copy-start | bytes 12582916 | tf_op jit(solution)/shard_map/while
  310.1 3.6 %copy-start.4 = (bf16[2048,64]{1,0:T(8,128)(2,1)S(1)}, bf16[2048,64]{1,0:T(8,128)(2,1)}, u32[]{:S(2)}) copy-start(bf16[2048,64]{1,0:T(8,128)(2,1)} %get-tuple-element.299) | copy-start | bytes 786436 | tf_op jit(solution)/shard_map/while
  313.6 1.7 copy-start.6
Sparse Core Ops, SparseCore 0:
  11.0 70.9 all-gather.5
  85.0 96.0 all-gather.3
